TPU v7x, 32 devices: a whole 2x2x4 slice. The times are simulated.
32 devices in a mesh: sub: 8 (over z, x), grp: 4 (over y, core).
Axes of the slice: x: 2, y: 2, z: 4, core: 2. Of those that a mesh axis runs over, the one named last changes fastest.
Arguments:
- solution: float32 [32, 128, 2048], P(('sub', 'grp')), may hold values from -6 to 6
- residual: float32 [32, 128, 2048], P(('sub', 'grp'))
- direction: float32 [32, 128, 2048], P(('sub', 'grp'))
- residual_product: float32 [128], replicated, may hold values from 65536 to 1310720
- neighbor_slots: int32 [32, 4], P(('sub', 'grp')), may hold values from 0 to 3, each once within a row
- coupling: bfloat16 [32, 96, 256, 128], P(('sub', 'grp')), may hold values from -0.375 to 0.375
- dirichlet_factor: bfloat16 [32, 96, 128, 128], P(('sub', 'grp')), may hold values from -0.5 to 0.5
- face_block: bfloat16 [32, 32, 128, 128], P(('sub', 'grp')), as said below
- neumann_factor: bfloat16 [32, 32, 128, 128], P(('sub', 'grp')), may hold values from -0.5 to 0.5
- primal_block: int32 [32, 128], P(('sub', 'grp')), may hold values from 0 to 31
- primal_basis: bfloat16 [32, 128, 128], P(('sub', 'grp')), may hold values from -1.5 to 1.5
- coarse_matrix: float32 [32, 9, 128, 128], P(('sub', 'grp')), may hold values from -0.17677669 to 0.17677669
- coarse_block_inverse: float32 [32, 128, 128], P(('sub', 'grp')), may hold values from -0.5 to 0.5
- coarse_pattern: int32 [32, 9], P(('sub', 'grp')), may hold values from 0 to 31, as said below
Outputs:
- new_solution: float32 [32, 128, 2048], P(('sub', 'grp'))
- new_residual: float32 [32, 128, 2048], P(('sub', 'grp'))
- new_direction: float32 [32, 128, 2048], P(('sub', 'grp'))
- new_product: float32 [128], replicated
Inputs may be any that keep to these rules, and one draw needn't show every extreme that they name: `neighbor_slots`: each row orders the four local face slots: entry d is the slot of the face toward direction d (sub lower, sub upper, grp lower, grp upper). `coarse_pattern`: row t names 9 different subdomains, the first of them t itself; subdomain s lies on the device of index s along sub+grp, and every entry lies within 2 positions of row t along sub, cyclically. `face_block`: each block is symmetric with every eigenvalue at least 0.5.
All inputs are finite; a program needn't handle non-finite values.
Results may differ from a plain program's by a relative error of at most 0.0003.
Values sent between devices are 32-bit elements; how exact they have to be, the bound alone decides.
A program may use at most 128 MiB of HBM per device.

v0:
```python
import jax
import jax.numpy as jnp
from jax import lax
from jax.sharding import PartitionSpec as P

REACH_SUBS = 2
highest_precision = lax.Precision.HIGHEST


def shifted(value, axis, steps):
    count = lax.axis_size(axis)
    pairs = [(source, (source + steps) % count) for source in range(count)]
    return lax.ppermute(value, axis, pairs)


def slot_table(neighbor_slots):
    return (neighbor_slots[0][:, None] == jnp.arange(4, dtype=jnp.int32)[None, :]).astype(
        jnp.float32
    )


def place_faces(directed, slot_onehot, block_width):
    load_count = directed.shape[1]
    face_width = directed.shape[2]
    placed = jnp.einsum("dk,dlf->lkf", slot_onehot, directed, precision=highest_precision)
    return placed.reshape(load_count, 4 * face_width // block_width, block_width)


def spread(owned_part, slot_onehot, block_width):
    face_width = owned_part.shape[2] // 2
    own_sub = owned_part[:, :, :face_width]
    own_grp = owned_part[:, :, face_width:]
    from_sub = shifted(own_sub, "sub", 1)
    from_grp = shifted(own_grp, "grp", 1)
    directed = jnp.stack([from_sub[0], own_sub[0], from_grp[0], own_grp[0]], 0)
    return place_faces(directed, slot_onehot, block_width)


def collect(local_part, slot_onehot):
    load_count = local_part.shape[0]
    placed = local_part.reshape(load_count, 4, -1)
    directed = jnp.einsum("dk,lkf->dlf", slot_onehot, placed, precision=highest_precision)
    to_sub = shifted(directed[0][None], "sub", -1)
    to_grp = shifted(directed[2][None], "grp", -1)
    owned_sub = directed[1][None] + to_sub
    owned_grp = directed[3][None] + to_grp
    return jnp.concatenate([owned_sub, owned_grp], 2)


def condensed(vector, couple, dirichlet, face_matrix):
    count_of_blocks = vector.shape[1]
    block_width = vector.shape[2]
    paired = jnp.concatenate(
        [
            jnp.concatenate([vector, jnp.roll(vector, -(offset + 1), axis=1)], 2)
            for offset in range(3)
        ],
        1,
    )
    interior = jnp.einsum("lib,ibk->lik", paired, couple, precision=highest_precision)
    middle = jnp.einsum("lik,ikm->lim", interior, dirichlet, precision=highest_precision)
    solved = jnp.einsum("lim,ikm->lik", middle, dirichlet, precision=highest_precision)
    returned = jnp.einsum("lik,ibk->lib", solved, couple, precision=highest_precision)
    result = jnp.einsum("ljb,jbk->ljk", vector, face_matrix, precision=highest_precision)
    for offset in range(3):
        portion = returned[:, offset * count_of_blocks : (offset + 1) * count_of_blocks]
        result = (
            result
            + portion[:, :, :block_width]
            + jnp.roll(portion[:, :, block_width:], offset + 1, axis=1)
        )
    return result


def coarse_neighbors(initial_step, pattern, matrix):
    load_count, primal_count = initial_step.shape
    grp_count = lax.axis_size("grp")
    sub_count = lax.axis_size("sub")
    reach_count = 2 * REACH_SUBS + 1
    entry_sub = pattern // grp_count
    entry_grp = pattern % grp_count
    position = (entry_sub - lax.axis_index("sub") + REACH_SUBS) % sub_count
    column = lax.all_gather(initial_step[None], "grp", axis=0, tiled=True)
    pieces = []
    for place in range(reach_count):
        if place == REACH_SUBS:
            pieces.append(column)
        else:
            pieces.append(shifted(column, "sub", REACH_SUBS - place))
    window = jnp.stack(pieces, 0).reshape(-1, load_count, primal_count)
    slot_index = position * grp_count + entry_grp
    chooser = (slot_index[:, None] == jnp.arange(window.shape[0], dtype=jnp.int32)[None, :]).astype(
        jnp.float32
    )
    chosen = jnp.einsum("kj,jlc->klc", chooser, window, precision=highest_precision)
    return jnp.einsum("klc,kcd->ld", chosen, matrix, precision=highest_precision)


def precondition(
    local_copy, slot_onehot, neumann, block_ids, primal_rows, matrix, inverse, pattern
):
    halved = local_copy * 0.5
    neumann_step = jnp.einsum("ljb,jbk->ljk", halved, neumann, precision=highest_precision)
    local_solve = jnp.einsum("ljk,jmk->ljm", neumann_step, neumann, precision=highest_precision)
    selector = (block_ids[:, None] == jnp.arange(halved.shape[1], dtype=jnp.int32)[None, :]).astype(
        jnp.float32
    )
    picked = jnp.einsum("ljb,cj->lcb", halved, selector, precision=highest_precision)
    coarse_residual = jnp.einsum("lcb,cb->lc", picked, primal_rows, precision=highest_precision)
    initial_step = jnp.dot(coarse_residual, inverse, precision=highest_precision)
    adjacent_sum = coarse_neighbors(initial_step, pattern, matrix)
    coarse_correction = initial_step + jnp.dot(
        coarse_residual - adjacent_sum, inverse, precision=highest_precision
    )
    weighted = coarse_correction[:, :, None] * primal_rows[None]
    spread_back = jnp.einsum("lcb,cj->ljb", weighted, selector, precision=highest_precision)
    return collect(0.5 * (local_solve + spread_back), slot_onehot)


def shards(
    solution,
    residual,
    direction,
    residual_product,
    neighbor_slots,
    coupling,
    dirichlet_factor,
    face_block,
    neumann_factor,
    primal_block,
    primal_basis,
    coarse_matrix,
    coarse_block_inverse,
    coarse_pattern,
):
    slot_onehot = slot_table(neighbor_slots)
    block_width = face_block.shape[2]
    couple = coupling[0].astype(jnp.float32)
    dirichlet = dirichlet_factor[0].astype(jnp.float32)
    face_matrix = face_block[0].astype(jnp.float32)
    neumann = neumann_factor[0].astype(jnp.float32)
    primal_rows = primal_basis[0].astype(jnp.float32)
    direction_local = spread(direction, slot_onehot, block_width)
    image = collect(condensed(direction_local, couple, dirichlet, face_matrix), slot_onehot)
    curvature = lax.psum(jnp.sum(direction * image, axis=(0, 2)), ("sub", "grp"))
    step_length = residual_product / curvature
    new_residual = residual - step_length[None, :, None] * image
    new_local = spread(new_residual, slot_onehot, block_width)
    preconditioned = precondition(
        new_local,
        slot_onehot,
        neumann,
        primal_block[0],
        primal_rows,
        coarse_matrix[0],
        coarse_block_inverse[0],
        coarse_pattern[0],
    )
    new_product = lax.psum(jnp.sum(new_residual * preconditioned, axis=(0, 2)), ("sub", "grp"))
    new_solution = solution + step_length[None, :, None] * direction
    step_ratio = new_product / residual_product
    new_direction = preconditioned + step_ratio[None, :, None] * direction
    return (new_solution, new_residual, new_direction, new_product)


def solution(mesh):
    in_specs = (
        P(("sub", "grp"), None, None),
        P(("sub", "grp"), None, None),
        P(("sub", "grp"), None, None),
        P(),
        P(("sub", "grp"), None),
        P(("sub", "grp"), None, None, None),
        P(("sub", "grp"), None, None, None),
        P(("sub", "grp"), None, None, None),
        P(("sub", "grp"), None, None, None),
        P(("sub", "grp"), None),
        P(("sub", "grp"), None, None),
        P(("sub", "grp"), None, None, None),
        P(("sub", "grp"), None, None),
        P(("sub", "grp"), None),
    )
    out_specs = (
        P(("sub", "grp"), None, None),
        P(("sub", "grp"), None, None),
        P(("sub", "grp"), None, None),
        P(),
    )
    return jax.shard_map(shards, mesh=mesh, in_specs=in_specs, out_specs=out_specs, check_vma=False)
```

profile of v0, /device:TPU:0, one launch (start us, length us, event | category | flops | bytes accessed | tf_op | source)
XLA Modules:
  0.0 302.8 jit_solution(3611158063502701570)
XLA Ops:
  2.6 3.0 collective-permute-start
  6.3 14.4 %collective-permute-done = f32[1,128,1024]{2,0,1:T(1,128)S(1)} collective-permute-done((f32[1,128,1024]{2,0,1:T(1,128)S(1)}, f32[1,128,1024]{2,0,1:T(1,128)S(1)}, u32[]{:S(2)}, u32[]{:S(2)}) %collective-permute-start) | collective-permute-done | bytes 524320 | tf_op jit(solution)/shard_map/ppermute | solution.py:13
  20.6 5.2 %fusion.45 = f32[128,4,1024]{2,1,0:T(4,128)} fusion(f32[1,128,1024]{2,0,1:T(1,128)S(1)} %copy.71, f32[1,128,1024]{2,0,1:T(1,128)S(1)} %collective-permute-done.1, f32[1,128,1024]{2,0,1:T(1,128)S(1)} %copy.70, f32[1,128,1024]{2,0,1:T(1,128)S(1)} %collective-permute-done, s32[4]{0:T(128)S(1)} %bitcast.127), kind=kOutput, calls=%fused_computation.46 | convolution fusion | flops 26738704 | bytes 4194320 | tf_op jit(solution)/shard_map/dk,dlf->lkf/dot_general | solution.py:25
  25.8 3.0 %reshape.139 = f32[128,32,128]{2,1,0:T(8,128)} reshape(f32[128,4,1024]{2,1,0:T(4,128)} %fusion.45) | data formatting | bytes 4194304 | tf_op jit(solution)/shard_map/reshape | solution.py:26
  31.9 6.1 %maximum_maximum_fusion = f32[128,96,256]{2,1,0:T(8,128)} fusion(f32[128,3,128]{2,1,0:T(4,128)S(1)} %slice.143, f32[128,29,128]{2,1,0:T(8,128)S(1)} %slice.142, f32[128,32,128]{2,1,0:T(8,128)S(1)} %copy-done.2, f32[128,2,128]{2,1,0:T(2,128)S(1)} %slice.141, f32[128,30,128]{2,1,0:T(8,128)S(1)} %slice.140, f32[128,1,128]{2,1,0:T(1,128)S(1)} %slice.139, ...), kind=kLoop, calls=%fused_computation | loop fusion | flops 25165824 | bytes 20971520 | tf_op jit(solution)/shard_map/concatenate | solution.py:53
  37.9 21.7 %fusion = f32[96,128,128]{2,1,0:T(8,128)} fusion(f32[128,96,256]{2,1,0:T(8,128)} %maximum_maximum_fusion, bf16[1,96,256,128]{3,2,1,0:T(8,128)(2,1)} %param.19), kind=kOutput, calls=%fused_computation.1 | convolution fusion | flops 4831838208 | bytes 25165824 | tf_op jit(solution)/shard_map/lib,ibk->lik/dot_general | solution.py:60
  59.6 5.3 %fusion.11 = f32[96,128,128]{2,1,0:T(8,128)S(1)} fusion(f32[96,128,128]{2,1,0:T(8,128)} %fusion, bf16[1,96,128,128]{3,2,1,0:T(8,128)(2,1)S(1)} %copy-done), kind=kOutput, calls=%fused_computation.12 | convolution fusion | flops 2415919104 | bytes 15728640 | tf_op jit(solution)/shard_map/lik,ikm->lim/dot_general | solution.py:61
  64.9 8.5 %fusion.9 = f32[96,128,128]{2,1,0:T(8,128)} fusion(f32[96,128,128]{2,1,0:T(8,128)S(1)} %fusion.11, bf16[1,96,128,128]{3,2,1,0:T(8,128)(2,1)S(1)} %copy-done), kind=kOutput, calls=%fused_computation.10 | convolution fusion | flops 2415919104 | bytes 15728640 | tf_op jit(solution)/shard_map/lim,ikm->lik/dot_general | solution.py:62
  73.4 8.4 %fusion.15 = f32[128,96,256]{0,2,1:T(8,128)S(1)} fusion(bf16[1,96,256,128]{3,2,1,0:T(8,128)(2,1)} %param.19, f32[96,128,128]{2,1,0:T(8,128)} %fusion.9), kind=kOutput, calls=%fused_computation.16 | convolution fusion | flops 4831838208 | bytes 25165824 | tf_op jit(solution)/shard_map/lik,ibk->lib/dot_general | solution.py:63
  84.0 5.4 %fusion.24 = f32[128,32,128]{0,2,1:T(8,128)} fusion(f32[128,96,256]{0,2,1:T(8,128)S(1)} %fusion.15, f32[128,31,128]{0,2,1:T(8,128)S(1)} %slice.146, f32[128,1,128]{0,2,1:T(8,128)S(1)} %slice.145, f32[128,30,128]{0,2,1:T(8,128)S(1)} %slice.149, f32[128,2,128]{0,2,1:T(8,128)S(1)} %slice.148, f32[128,29,128]{0,2,1:T(8,128)S(1)} %slice.152, ...), kind=kOutput, calls=%fused_computation.22 | convolution fusion | flops 810024960 | bytes 17825792 | tf_op jit(solution)/shard_map/ljb,jbk->ljk/dot_general | solution.py:64
  89.5 3.3 %copy.44 = f32[128,4,1024]{2,1,0:T(4,128)} copy(f32[128,4,1024]{0,2,1:T(8,128)} %bitcast.117) | data formatting | bytes 4194304 | tf_op jit(solution)/shard_map/reshape | solution.py:41
  92.7 3.7 %fusion.82 = f32[4,128,1024]{2,0,1:T(4,128)S(1)} fusion(f32[128,4,1024]{2,1,0:T(4,128)} %copy.44, s32[4]{0:T(128)S(1)} %bitcast.128), kind=kOutput, calls=%fused_computation.102 | convolution fusion | flops 25165840 | bytes 4194320 | tf_op jit(solution)/shard_map/dk,lkf->dlf/dot_general | solution.py:42
  100.0 11.2 %collective-permute-done.2 = f32[1,128,1024]{2,1,0:T(8,128)S(1)} collective-permute-done((f32[1,128,1024]{2,1,0:T(8,128)S(1)}, f32[1,128,1024]{2,1,0:T(8,128)S(1)}, u32[]{:S(2)}, u32[]{:S(2)}) %collective-permute-start.2) | collective-permute-done | bytes 524320 | tf_op jit(solution)/shard_map/ppermute | solution.py:13
  111.7 39.6 %psum.14 = f32[128]{0:T(128)S(1)} all-reduce(f32[128]{0:T(128)S(1)} %multiply_reduce_fusion.1), channel_id=1, replica_groups=mesh['sub'=8,'grp'=4] {'sub','grp'}, use_global_device_ids=true, to_apply=%region_1.2 | all-reduce | flops 128 | bytes 1024 | tf_op jit(solution)/shard_map/psum | solution.py:145
  155.2 13.2 %collective-permute-done.4 = f32[1,128,1024]{2,1,0:T(8,128)S(1)} collective-permute-done((f32[1,128,1024]{2,1,0:T(8,128)S(1)}, f32[1,128,1024]{2,1,0:T(8,128)S(1)}, u32[]{:S(2)}, u32[]{:S(2)}) %collective-permute-start.4) | collective-permute-done | bytes 524320 | tf_op jit(solution)/shard_map/ppermute | solution.py:13
  171.0 4.8 %multiply_bitcast_fusion = f32[128,4,1024]{2,1,0:T(4,128)} fusion(f32[4,128,1024]{2,1,0:T(8,128)S(1)} %pad_maximum_fusion, s32[4]{0:T(128)S(1)} %bitcast.129), kind=kOutput, calls=%fused_computation.45 | convolution fusion | flops 25690128 | bytes 4194320 | tf_op jit(solution)/shard_map/dk,dlf->lkf/dot_general | solution.py:25
  175.8 2.5 mul.80
  178.3 3.5 %fusion.66 = f32[128,128,128]{2,0,1:T(8,128)S(1)} fusion(f32[128,32,128]{2,1,0:T(8,128)S(1)} %mul.80, s32[128]{0:T(128)S(1)} %bitcast.131), kind=kOutput, calls=%fused_computation.79 | convolution fusion | flops 805310464 | bytes 10486272 | tf_op jit(solution)/shard_map/ljb,cj->lcb/dot_general | solution.py:108
  181.8 11.0 %fusion.2 = f32[128,1,128]{2,1,0:T(1,128)S(1)} fusion(f32[128,128,128]{2,0,1:T(8,128)S(1)} %fusion.66, bf16[128,128,1]{1,0,2:T(8,128)(2,1)S(1)} %bitcast.126), kind=kOutput, calls=%fused_computation.3 | convolution fusion | flops 25165824 | bytes 8486912 | tf_op jit(solution)/shard_map/lcb,cb->lc/dot_general | solution.py:109
  193.1 5.8 %all-gather = f32[512,128]{1,0:T(8,128)S(1)} all-gather(f32[128,128]{1,0:T(8,128)S(1)} %fusion.61), channel_id=2, replica_groups=mesh['sub'=8,'grp'=4] {'grp'}, dimensions={0}, use_global_device_ids=true | all-gather | bytes 327680 | tf_op jit(solution)/shard_map/all_gather | solution.py:83
  199.6 4.3 %collective-permute-start.8 = (f32[4,128,128]{2,1,0:T(8,128)S(1)}, f32[4,128,128]{2,1,0:T(8,128)S(1)}, u32[]{:S(2)}, u32[]{:S(2)}) collective-permute-start(f32[4,128,128]{2,1,0:T(8,128)S(1)} %bitcast.121), channel_id=1, source_target_pairs={{0,28},{4,0},{8,4},{12,8},{16,12},{20,16},{24,20},{28,24},{1,29},{... | collective-permute-start | bytes 786440 | tf_op jit(solution)/shard_map/ppermute | solution.py:13
  205.6 3.6 %fusion.37 = f32[32,128,128]{2,1,0:T(8,128)} fusion(f32[128,32,128]{2,1,0:T(8,128)S(1)} %mul.80, bf16[1,32,128,128]{3,2,1,0:T(8,128)(2,1)S(1)} %copy-done.9), kind=kOutput, calls=%fused_computation.38 | convolution fusion | flops 805306368 | bytes 5242880 | tf_op jit(solution)/shard_map/ljb,jbk->ljk/dot_general | solution.py:103
  210.0 3.6 %collective-permute-done.7 = f32[4,128,128]{2,1,0:T(8,128)S(1)} collective-permute-done((f32[4,128,128]{2,1,0:T(8,128)S(1)}, f32[4,128,128]{2,1,0:T(8,128)S(1)}, u32[]{:S(2)}, u32[]{:S(2)}) %collective-permute-start.7) | collective-permute-done | bytes 262176 | tf_op jit(solution)/shard_map/ppermute | solution.py:13
  213.9 6.6 %collective-permute-done.9 = f32[4,128,128]{2,1,0:T(8,128)S(1)} collective-permute-done((f32[4,128,128]{2,1,0:T(8,128)S(1)}, f32[4,128,128]{2,1,0:T(8,128)S(1)}, u32[]{:S(2)}, u32[]{:S(2)}) %collective-permute-start.9) | collective-permute-done | bytes 262176 | tf_op jit(solution)/shard_map/ppermute | solution.py:13
  223.5 5.3 %fusion.5 = f32[32,128,128]{2,0,1:T(8,128)} fusion(f32[128,128]{1,0:T(8,128)S(1)} %bitcast_convert_fusion, f32[128,128]{1,0:T(8,128)S(1)} %convolution_add_fusion, s32[128]{0:T(128)S(1)} %bitcast.132), kind=kOutput, calls=%fused_computation.6 | convolution fusion | flops 807407616 | bytes 2228736 | tf_op jit(solution)/shard_map/lcb,cj->ljb/dot_general | solution.py:116
  228.8 3.1 %copy.51 = f32[32,128,128]{1,2,0:T(8,128)} copy(f32[32,128,128]{2,0,1:T(8,128)} %fusion.5) | data formatting | bytes 4194304 | tf_op jit(solution)/shard_map/lcb,cj->ljb/dot_general | solution.py:116
  231.9 5.5 %add_multiply_fusion = f32[32,128,128]{1,2,0:T(8,128)} fusion(f32[32,128,128]{1,2,0:T(8,128)} %copy.51, f32[32,128,128]{2,1,0:T(8,128)S(1)} %copy-done.6, bf16[1,32,128,128]{3,2,1,0:T(8,128)(2,1)} %param.22), kind=kOutput, calls=%fused_computation.44 | convolution fusion | flops 806354944 | bytes 7340032 | tf_op jit(solution)/shard_map/ljk,jmk->ljm/dot_general | solution.py:104
  237.4 3.1 %copy.52 = f32[128,4,1024]{2,1,0:T(4,128)} copy(f32[128,4,1024]{0,2,1:T(8,128)} %bitcast.116) | data formatting | bytes 4194304 | tf_op jit(solution)/shard_map/reshape | solution.py:41
  240.6 3.7 %fusion.80 = f32[4,128,1024]{2,0,1:T(4,128)S(1)} fusion(f32[128,4,1024]{2,1,0:T(4,128)} %copy.52, s32[4]{0:T(128)S(1)} %bitcast.130), kind=kOutput, calls=%fused_computation.101 | convolution fusion | flops 25165840 | bytes 4194320 | tf_op jit(solution)/shard_map/dk,lkf->dlf/dot_general | solution.py:42
  247.0 12.8 %collective-permute-done.10 = f32[1,128,1024]{2,1,0:T(8,128)S(1)} collective-permute-done((f32[1,128,1024]{2,1,0:T(8,128)S(1)}, f32[1,128,1024]{2,1,0:T(8,128)S(1)}, u32[]{:S(2)}, u32[]{:S(2)}) %collective-permute-start.10) | collective-permute-done | bytes 524320 | tf_op jit(solution)/shard_map/ppermute | solution.py:13
  260.9 38.0 %psum.15 = f32[128]{0:T(128)S(1)} all-reduce(f32[128]{0:T(128)S(1)} %multiply_reduce_fusion), channel_id=1, replica_groups=mesh['sub'=8,'grp'=4] {'sub','grp'}, use_global_device_ids=true, to_apply=%region_3.4 | all-reduce | flops 128 | bytes 1024 | tf_op jit(solution)/shard_map/psum | solution.py:159
  299.0 3.6 %multiply_add_fusion = (f32[1,128,2048]{2,1,0:T(8,128)}, f32[1,128,2048]{2,1,0:T(8,128)}) fusion(f32[1,128,2048]{2,1,0:T(8,128)} %param.16, f32[1,128,1024]{2,1,0:T(8,128)} %copy-done.8, f32[1,128,1024]{2,1,0:T(8,128)} %copy-done.7, f32[128]{0:T(128)S(1)} %div.23, f32[1,128,2048]{2,1,0:T(8,128)} %param.14, f32[128]{0:T(128)S(1)} %div.18), kind=kLoop, calls=%fused_computation.57 | loop fusion | flops 1310720 | bytes 5243904 | tf_op jit(solution)/shard_map/add | solution.py:162
  (103 shorter events, 28.7 us)
Async XLA Ops:
  0.6 59.0 %copy-start = (bf16[1,96,128,128]{3,2,1,0:T(8,128)(2,1)S(1)}, bf16[1,96,128,128]{3,2,1,0:T(8,128)(2,1)}, u32[]{:S(2)}) copy-start(bf16[1,96,128,128]{3,2,1,0:T(8,128)(2,1)} %param.20) | copy-start | bytes 9437188
  0.6 20.0 %copy-start.17 = (s32[1,4]{1,0:T(1,128)S(1)}, s32[1,4]{1,0:T(1,128)}, u32[]{:S(2)}) copy-start(s32[1,4]{1,0:T(1,128)} %param.18) | copy-start | bytes 52
  2.6 18.0 %collective-permute-start = (f32[1,128,1024]{2,0,1:T(1,128)S(1)}, f32[1,128,1024]{2,0,1:T(1,128)S(1)}, u32[]{:S(2)}, u32[]{:S(2)}) collective-permute-start(f32[1,128,1024]{2,0,1:T(1,128)S(1)} %copy.70), channel_id=1, source_target_pairs={{0,4},{4,8},{8,12},{12,16},{16,20},{20,24},{24,28},{28,0},{1,5},{5... | collective-permute-start | bytes 1572872 | tf_op jit(solution)/shard_map/ppermute | solution.py:13
  6.2 14.4 %collective-permute-start.1 = (f32[1,128,1024]{2,0,1:T(1,128)S(1)}, f32[1,128,1024]{2,0,1:T(1,128)S(1)}, u32[]{:S(2)}, u32[]{:S(2)}) collective-permute-start(f32[1,128,1024]{2,0,1:T(1,128)S(1)} %copy.71), channel_id=1, source_target_pairs={{0,1},{1,2},{2,3},{3,0},{4,5},{5,6},{6,7},{7,4},{8,9},{9,10},{10,1... | collective-permute-start | bytes 1572872 | tf_op jit(solution)/shard_map/ppermute | solution.py:13
  28.8 2.2 copy-start.2
  82.2 1.6 copy-start.3
  82.2 1.9 copy-start.12
  98.1 13.1 %collective-permute-start.2 = (f32[1,128,1024]{2,1,0:T(8,128)S(1)}, f32[1,128,1024]{2,1,0:T(8,128)S(1)}, u32[]{:S(2)}, u32[]{:S(2)}) collective-permute-start(f32[1,128,1024]{2,1,0:T(8,128)S(1)} %copy.73), channel_id=1, source_target_pairs={{0,28},{4,0},{8,4},{12,8},{16,12},{20,16},{24,20},{28,24},{1,29},{... | collective-permute-start | bytes 1572872 | tf_op jit(solution)/shard_map/ppermute | solution.py:13
  99.9 11.6 %copy-start.5 = (f32[1,128,2048]{2,1,0:T(8,128)S(1)}, f32[1,128,2048]{2,1,0:T(8,128)}, u32[]{:S(2)}) copy-start(f32[1,128,2048]{2,1,0:T(8,128)} %param.16) | copy-start | bytes 3145732
  100.0 11.4 %collective-permute-start.3 = (f32[1,128,1024]{2,1,0:T(8,128)S(1)}, f32[1,128,1024]{2,1,0:T(8,128)S(1)}, u32[]{:S(2)}, u32[]{:S(2)}) collective-permute-start(f32[1,128,1024]{2,1,0:T(8,128)S(1)} %copy.75), channel_id=1, source_target_pairs={{0,3},{1,0},{2,1},{3,2},{4,7},{5,4},{6,5},{7,6},{8,11},{9,8},{10,9... | collective-permute-start | bytes 1572872 | tf_op jit(solution)/shard_map/ppermute | solution.py:13
  111.3 39.9 %copy-start.20 = (f32[128]{0:T(128)S(1)}, f32[128]{0:T(128)}, u32[]{:S(2)}) copy-start(f32[128]{0:T(128)} %param.17) | copy-start | bytes 1540
  151.3 3.9 %copy-start.19 = (s32[1,9]{1,0:T(1,128)S(1)}, s32[1,9]{1,0:T(1,128)}, u32[]{:S(2)}) copy-start(s32[1,9]{1,0:T(1,128)} %param.27) | copy-start | bytes 112
  151.3 3.9 %copy-start.15 = (bf16[1,128,128]{2,1,0:T(8,128)(2,1)S(1)}, bf16[1,128,128]{2,1,0:T(8,128)(2,1)}, u32[]{:S(2)}) copy-start(bf16[1,128,128]{2,1,0:T(8,128)(2,1)} %param.24) | copy-start | bytes 98308
  152.7 107.4 %copy-start.4 = (f32[1,128,2048]{2,1,0:T(8,128)}, f32[1,128,2048]{2,1,0:T(8,128)S(1)}, u32[]{:S(2)}) copy-start(f32[1,128,2048]{2,1,0:T(8,128)S(1)} %multiply_subtract_fusion) | copy-start | bytes 3145732
  152.8 15.6 %copy-start.10 = (f32[1,128,1024]{2,1,0:T(8,128)}, f32[1,128,1024]{2,1,0:T(8,128)S(1)}, u32[]{:S(2)}) copy-start(f32[1,128,1024]{2,1,0:T(8,128)S(1)} %get-tuple-element.18) | copy-start | bytes 1572868
  152.8 15.6 %copy-start.11 = (f32[1,128,1024]{2,1,0:T(8,128)}, f32[1,128,1024]{2,1,0:T(8,128)S(1)}, u32[]{:S(2)}) copy-start(f32[1,128,1024]{2,1,0:T(8,128)S(1)} %get-tuple-element.19) | copy-start | bytes 1572868
  152.8 15.6 %collective-permute-start.4 = (f32[1,128,1024]{2,1,0:T(8,128)S(1)}, f32[1,128,1024]{2,1,0:T(8,128)S(1)}, u32[]{:S(2)}, u32[]{:S(2)}) collective-permute-start(f32[1,128,1024]{2,1,0:T(8,128)S(1)} %get-tuple-element.18), channel_id=1, source_target_pairs={{0,4},{4,8},{8,12},{12,16},{16,20},{20,24},{24,28},{28,0},{1,5},{5... | collective-permute-start | bytes 1572872 | tf_op jit(solution)/shard_map/ppermute | solution.py:13
  155.2 14.1 %collective-permute-start.5 = (f32[1,128,1024]{2,1,0:T(8,128)S(1)}, f32[1,128,1024]{2,1,0:T(8,128)}, u32[]{:S(2)}, u32[]{:S(2)}) collective-permute-start(f32[1,128,1024]{2,1,0:T(8,128)S(1)} %get-tuple-element.19), channel_id=1, source_target_pairs={{0,1},{1,2},{2,3},{3,0},{4,5},{5,6},{6,7},{7,4},{8,9},{9,10},{10,1... | collective-permute-start | bytes 1572872 | tf_op jit(solution)/shard_map/ppermute | solution.py:13
  175.8 2.5 copy-start.18
  181.8 11.0 %copy-start.16 = (f32[1,128,128]{2,1,0:T(8,128)S(1)}, f32[1,128,128]{2,1,0:T(8,128)}, u32[]{:S(2)}) copy-start(f32[1,128,128]{2,1,0:T(8,128)} %param.26) | copy-start | bytes 196612
  181.8 23.8 %copy-start.9 = (bf16[1,32,128,128]{3,2,1,0:T(8,128)(2,1)S(1)}, bf16[1,32,128,128]{3,2,1,0:T(8,128)(2,1)}, u32[]{:S(2)}) copy-start(bf16[1,32,128,128]{3,2,1,0:T(8,128)(2,1)} %param.22) | copy-start | bytes 3145732
  198.9 11.1 %collective-permute-start.6 = (f32[4,128,128]{2,1,0:T(8,128)S(1)}, f32[4,128,128]{2,1,0:T(8,128)S(1)}, u32[]{:S(2)}, u32[]{:S(2)}) collective-permute-start(f32[4,128,128]{2,1,0:T(8,128)S(1)} %bitcast.119), channel_id=1, source_target_pairs={{0,8},{4,12},{8,16},{12,20},{16,24},{20,28},{24,0},{28,4},{1,9},{5... | collective-permute-start | bytes 786440 | tf_op jit(solution)/shard_map/ppermute | solution.py:13
  199.2 14.4 %collective-permute-start.7 = (f32[4,128,128]{2,1,0:T(8,128)S(1)}, f32[4,128,128]{2,1,0:T(8,128)S(1)}, u32[]{:S(2)}, u32[]{:S(2)}) collective-permute-start(f32[4,128,128]{2,1,0:T(8,128)S(1)} %bitcast.120), channel_id=1, source_target_pairs={{0,4},{4,8},{8,12},{12,16},{16,20},{20,24},{24,28},{28,0},{1,5},{5... | collective-permute-start | bytes 786440 | tf_op jit(solution)/shard_map/ppermute | solution.py:13
  199.6 14.3 %collective-permute-start.8 = (f32[4,128,128]{2,1,0:T(8,128)S(1)}, f32[4,128,128]{2,1,0:T(8,128)S(1)}, u32[]{:S(2)}, u32[]{:S(2)}) collective-permute-start(f32[4,128,128]{2,1,0:T(8,128)S(1)} %bitcast.121), channel_id=1, source_target_pairs={{0,28},{4,0},{8,4},{12,8},{16,12},{20,16},{24,20},{28,24},{1,29},{... | collective-permute-start | bytes 786440 | tf_op jit(solution)/shard_map/ppermute | solution.py:13
  203.9 16.6 %collective-permute-start.9 = (f32[4,128,128]{2,1,0:T(8,128)S(1)}, f32[4,128,128]{2,1,0:T(8,128)S(1)}, u32[]{:S(2)}, u32[]{:S(2)}) collective-permute-start(f32[4,128,128]{2,1,0:T(8,128)S(1)} %bitcast.122), channel_id=1, source_target_pairs={{0,24},{4,28},{8,0},{12,4},{16,8},{20,12},{24,16},{28,20},{1,25},{... | collective-permute-start | bytes 786440 | tf_op jit(solution)/shard_map/ppermute | solution.py:13
  213.6 8.4 %copy-start.13 = (f32[1,9,128,128]{3,2,1,0:T(8,128)S(1)}, f32[1,9,128,128]{3,2,1,0:T(8,128)}, u32[]{:S(2)}) copy-start(f32[1,9,128,128]{3,2,1,0:T(8,128)} %param.25) | copy-start | bytes 1769476
  228.8 3.1 %copy-start.6 = (f32[32,128,128]{2,1,0:T(8,128)S(1)}, f32[32,128,128]{2,1,0:T(8,128)}, u32[]{:S(2)}) copy-start(f32[32,128,128]{2,1,0:T(8,128)} %fusion.37) | copy-start | bytes 6291460
  245.9 13.9 %collective-permute-start.10 = (f32[1,128,1024]{2,1,0:T(8,128)S(1)}, f32[1,128,1024]{2,1,0:T(8,128)S(1)}, u32[]{:S(2)}, u32[]{:S(2)}) collective-permute-start(f32[1,128,1024]{2,1,0:T(8,128)S(1)} %copy.77), channel_id=1, source_target_pairs={{0,28},{4,0},{8,4},{12,8},{16,12},{20,16},{24,20},{28,24},{1,29},{... | collective-permute-start | bytes 1572872 | tf_op jit(solution)/shard_map/ppermute | solution.py:13
  246.2 13.8 %collective-permute-start.11 = (f32[1,128,1024]{2,1,0:T(8,128)S(1)}, f32[1,128,1024]{2,1,0:T(8,128)S(1)}, u32[]{:S(2)}, u32[]{:S(2)}) collective-permute-start(f32[1,128,1024]{2,1,0:T(8,128)S(1)} %copy.79), channel_id=1, source_target_pairs={{0,3},{1,0},{2,1},{3,2},{4,7},{5,4},{6,5},{7,6},{8,11},{9,8},{10,9... | collective-permute-start | bytes 1572872 | tf_op jit(solution)/shard_map/ppermute | solution.py:13
  260.1 0.9 copy-start.8
  299.0 3.6 %copy-start.21 = (f32[128]{0:T(128)}, f32[128]{0:T(128)S(1)}, u32[]{:S(2)}) copy-start(f32[128]{0:T(128)S(1)} %psum.15) | copy-start | bytes 1540
  299.0 3.6 %copy-start.1 = (bf16[1,96,128,128]{3,2,1,0:T(8,128)(2,1)S(1)}, bf16[1,96,128,128]{3,2,1,0:T(8,128)(2,1)}, u32[]{:S(2)}) copy-start(bf16[1,96,128,128]{3,2,1,0:T(8,128)(2,1)} %param.20) | copy-start | bytes 9437188
  (2 other events, 1.6 us)
where the time goes:
time: 308 us; the launch traced here: 303 us
  matrix products  98.6 us (32%)
  blocking collectives  83.4 us (27%)
  waiting for transfers between devices  62.8 us (20%)
  local copies, waits for them, and re-layouts  27.9 us (9%)
  starting transfers between devices  14.9 us (5%)
  other arithmetic  13.7 us (4%)
    ppermute x12, waiting for transfers between devices, shifted(): return lax.ppermute(value, axis, pairs)  62.8 us
    psum x1, blocking collectives, shards(): lax.psum(jnp.sum(direction * image, axis=(0, 2)), ('sub', 'grp'))  39.6 us
    psum x1, blocking collectives, shards(): lax.psum(jnp.sum(new_residual * preconditioned, axis=(0, 2)), ('sub', 'gr...  38 us
    dot_general x1, matrix products, condensed(): jnp.einsum('lib,ibk->lik', paired, couple, precision=highest_precision)  21.7 us
    ppermute x12, starting transfers between devices, shifted(): return lax.ppermute(value, axis, pairs)  14.9 us
    dot_general x1, matrix products, precondition(): jnp.einsum('lcb,cb->lc', picked, primal_rows, precision=highest_precision)  11 us
    dot_general x2, matrix products, place_faces(): jnp.einsum('dk,dlf->lkf', slot_onehot, directed, precision=highest_precis...  9.93 us
    dot_general x1, matrix products, condensed(): jnp.einsum('lim,ikm->lik', middle, dirichlet, precision=highest_precision)  8.47 us
  transfers between devices with their start and end apart: 12, of which 8 were waited for; matrix products, arithmetic and copies ran while one was open for 2% of the time, Pallas kernels for 0%

commit v1 on v0

--- a/solution.py
+++ b/solution.py
@@ -142,7 +142,9 @@
     primal_rows = primal_basis[0].astype(jnp.float32)
     direction_local = spread(direction, slot_onehot, block_width)
     image = collect(condensed(direction_local, couple, dirichlet, face_matrix), slot_onehot)
-    curvature = lax.psum(jnp.sum(direction * image, axis=(0, 2)), ("sub", "grp"))
+    curvature = jnp.sum(direction * image, axis=(0, 2))
+    for mesh_axis in ("grp", "sub"):
+        curvature = lax.psum(curvature, mesh_axis)
     step_length = residual_product / curvature
     new_residual = residual - step_length[None, :, None] * image
     new_local = spread(new_residual, slot_onehot, block_width)

time: 308 us -> 292 us (0.948)
  blocking collectives: 83.4 us -> 74.3 us
  waiting for transfers between devices: 62.8 us -> 56.7 us
    psum x1 -> x2, blocking collectives: 39.6 us -> 26.9 us  [shards(): curvature = lax.psum(curvature, mesh_axis)]
    ppermute x12, waiting for transfers between devices: 62.8 us -> 56.7 us  [shifted(): return lax.ppermute(value, axis, pairs)]
    psum x1, blocking collectives: 38 us -> 41.6 us  [shards(): lax.psum(jnp.sum(new_residual * preconditioned, axis=(0, 2)), ('sub', 'gr...]
where the time goes in v1:
time: 292 us; the launch traced here: 287 us
  matrix products  98.7 us (34%)
  blocking collectives  74.3 us (25%)
  waiting for transfers between devices  56.7 us (19%)
  local copies, waits for them, and re-layouts  27.9 us (10%)
  starting transfers between devices  13.9 us (5%)
  other arithmetic  13.7 us (5%)
    ppermute x12, waiting for transfers between devices, shifted(): return lax.ppermute(value, axis, pairs)  56.7 us
    psum x1, blocking collectives, shards(): lax.psum(jnp.sum(new_residual * preconditioned, axis=(0, 2)), ('sub', 'gr...  41.6 us
    psum x2, blocking collectives, shards(): curvature = lax.psum(curvature, mesh_axis)  26.9 us
    dot_general x1, matrix products, condensed(): jnp.einsum('lib,ibk->lik', paired, couple, precision=highest_precision)  21.7 us
    ppermute x12, starting transfers between devices, shifted(): return lax.ppermute(value, axis, pairs)  13.9 us
    dot_general x1, matrix products, precondition(): jnp.einsum('lcb,cb->lc', picked, primal_rows, precision=highest_precision)  11 us
    dot_general x2, matrix products, place_faces(): jnp.einsum('dk,dlf->lkf', slot_onehot, directed, precision=highest_precis...  9.95 us
    dot_general x1, matrix products, condensed(): jnp.einsum('lim,ikm->lik', middle, dirichlet, precision=highest_precision)  8.5 us
  transfers between devices with their start and end apart: 12, of which 8 were waited for; matrix products, arithmetic and copies ran while one was open for 2% of the time, Pallas kernels for 0%

profile of v1, /device:TPU:0, one launch (start us, length us, event | category | flops | bytes accessed | tf_op | source)
XLA Modules:
  0.0 286.8 jit_solution(5397140383038634646)
XLA Ops:
  2.6 3.0 %collective-permute-start = (f32[1,128,1024]{2,0,1:T(1,128)S(1)}, f32[1,128,1024]{2,0,1:T(1,128)S(1)}, u32[]{:S(2)}, u32[]{:S(2)}) collective-permute-start(f32[1,128,1024]{2,0,1:T(1,128)S(1)} %copy.70), channel_id=1, source_target_pairs={{0,4},{4,8},{8,12},{12,16},{16,20},{20,24},{24,28},{28,0},{1,5},{5... | collective-permute-start | bytes 1572872 | tf_op jit(solution)/shard_map/ppermute | solution.py:13
  6.3 14.4 %collective-permute-done = f32[1,128,1024]{2,0,1:T(1,128)S(1)} collective-permute-done((f32[1,128,1024]{2,0,1:T(1,128)S(1)}, f32[1,128,1024]{2,0,1:T(1,128)S(1)}, u32[]{:S(2)}, u32[]{:S(2)}) %collective-permute-start) | collective-permute-done | bytes 524320 | tf_op jit(solution)/shard_map/ppermute | solution.py:13
  20.6 5.2 %fusion.45 = f32[128,4,1024]{2,1,0:T(4,128)} fusion(f32[1,128,1024]{2,0,1:T(1,128)S(1)} %copy.71, f32[1,128,1024]{2,0,1:T(1,128)S(1)} %collective-permute-done.1, f32[1,128,1024]{2,0,1:T(1,128)S(1)} %copy.70, f32[1,128,1024]{2,0,1:T(1,128)S(1)} %collective-permute-done, s32[4]{0:T(128)S(1)} %bitcast.127), kind=kOutput, calls=%fused_computation.46 | convolution fusion | flops 26738704 | bytes 4194320 | tf_op jit(solution)/shard_map/dk,dlf->lkf/dot_general | solution.py:25
  25.8 3.1 %reshape.139 = f32[128,32,128]{2,1,0:T(8,128)} reshape(f32[128,4,1024]{2,1,0:T(4,128)} %fusion.45) | data formatting | bytes 4194304 | tf_op jit(solution)/shard_map/reshape | solution.py:26
  31.9 6.1 %maximum_maximum_fusion = f32[128,96,256]{2,1,0:T(8,128)} fusion(f32[128,3,128]{2,1,0:T(4,128)S(1)} %slice.143, f32[128,29,128]{2,1,0:T(8,128)S(1)} %slice.142, f32[128,32,128]{2,1,0:T(8,128)S(1)} %copy-done.2, f32[128,2,128]{2,1,0:T(2,128)S(1)} %slice.141, f32[128,30,128]{2,1,0:T(8,128)S(1)} %slice.140, f32[128,1,128]{2,1,0:T(1,128)S(1)} %slice.139, ...), kind=kLoop, calls=%fused_computation | loop fusion | flops 25165824 | bytes 20971520 | tf_op jit(solution)/shard_map/concatenate | solution.py:53
  38.0 21.7 %fusion = f32[96,128,128]{2,1,0:T(8,128)} fusion(f32[128,96,256]{2,1,0:T(8,128)} %maximum_maximum_fusion, bf16[1,96,256,128]{3,2,1,0:T(8,128)(2,1)} %param.19), kind=kOutput, calls=%fused_computation.1 | convolution fusion | flops 4831838208 | bytes 25165824 | tf_op jit(solution)/shard_map/lib,ibk->lik/dot_general | solution.py:60
  59.7 5.3 %fusion.11 = f32[96,128,128]{2,1,0:T(8,128)S(1)} fusion(f32[96,128,128]{2,1,0:T(8,128)} %fusion, bf16[1,96,128,128]{3,2,1,0:T(8,128)(2,1)S(1)} %copy-done), kind=kOutput, calls=%fused_computation.12 | convolution fusion | flops 2415919104 | bytes 15728640 | tf_op jit(solution)/shard_map/lik,ikm->lim/dot_general | solution.py:61
  65.0 8.5 %fusion.9 = f32[96,128,128]{2,1,0:T(8,128)} fusion(f32[96,128,128]{2,1,0:T(8,128)S(1)} %fusion.11, bf16[1,96,128,128]{3,2,1,0:T(8,128)(2,1)S(1)} %copy-done), kind=kOutput, calls=%fused_computation.10 | convolution fusion | flops 2415919104 | bytes 15728640 | tf_op jit(solution)/shard_map/lim,ikm->lik/dot_general | solution.py:62
  73.5 8.4 %fusion.15 = f32[128,96,256]{0,2,1:T(8,128)S(1)} fusion(bf16[1,96,256,128]{3,2,1,0:T(8,128)(2,1)} %param.19, f32[96,128,128]{2,1,0:T(8,128)} %fusion.9), kind=kOutput, calls=%fused_computation.16 | convolution fusion | flops 4831838208 | bytes 25165824 | tf_op jit(solution)/shard_map/lik,ibk->lib/dot_general | solution.py:63
  84.1 5.5 %fusion.24 = f32[128,32,128]{0,2,1:T(8,128)} fusion(f32[128,96,256]{0,2,1:T(8,128)S(1)} %fusion.15, f32[128,31,128]{0,2,1:T(8,128)S(1)} %slice.146, f32[128,1,128]{0,2,1:T(8,128)S(1)} %slice.145, f32[128,30,128]{0,2,1:T(8,128)S(1)} %slice.149, f32[128,2,128]{0,2,1:T(8,128)S(1)} %slice.148, f32[128,29,128]{0,2,1:T(8,128)S(1)} %slice.152, ...), kind=kOutput, calls=%fused_computation.22 | convolution fusion | flops 810024960 | bytes 17825792 | tf_op jit(solution)/shard_map/ljb,jbk->ljk/dot_general | solution.py:64
  89.6 3.2 %copy.44 = f32[128,4,1024]{2,1,0:T(4,128)} copy(f32[128,4,1024]{0,2,1:T(8,128)} %bitcast.117) | data formatting | bytes 4194304 | tf_op jit(solution)/shard_map/reshape | solution.py:41
  92.8 3.7 %fusion.82 = f32[4,128,1024]{2,0,1:T(4,128)S(1)} fusion(f32[128,4,1024]{2,1,0:T(4,128)} %copy.44, s32[4]{0:T(128)S(1)} %bitcast.128), kind=kOutput, calls=%fused_computation.102 | convolution fusion | flops 25165840 | bytes 4194320 | tf_op jit(solution)/shard_map/dk,lkf->dlf/dot_general | solution.py:42
  100.1 11.2 %collective-permute-done.2 = f32[1,128,1024]{2,1,0:T(8,128)S(1)} collective-permute-done((f32[1,128,1024]{2,1,0:T(8,128)S(1)}, f32[1,128,1024]{2,1,0:T(8,128)S(1)}, u32[]{:S(2)}, u32[]{:S(2)}) %collective-permute-start.2) | collective-permute-done | bytes 524320 | tf_op jit(solution)/shard_map/ppermute | solution.py:13
  111.8 5.7 %psum.21 = f32[128]{0:T(128)S(1)} all-reduce(f32[128]{0:T(128)S(1)} %multiply_reduce_fusion.1), channel_id=1, replica_groups=mesh['sub'=8,'grp'=4] {'grp'}, use_global_device_ids=true, to_apply=%region_1.2 | all-reduce | flops 128 | bytes 1024 | tf_op jit(solution)/shard_map/psum | solution.py:147
  117.5 21.2 %psum.22 = f32[128]{0:T(128)S(1)} all-reduce(f32[128]{0:T(128)S(1)} %psum.21), channel_id=1, replica_groups=mesh['sub'=8,'grp'=4] {'sub'}, use_global_device_ids=true, to_apply=%region_2.3 | all-reduce | flops 128 | bytes 1024 | tf_op jit(solution)/shard_map/psum | solution.py:147
  140.5 12.5 %collective-permute-done.4 = f32[1,128,1024]{2,1,0:T(8,128)S(1)} collective-permute-done((f32[1,128,1024]{2,1,0:T(8,128)S(1)}, f32[1,128,1024]{2,1,0:T(8,128)S(1)}, u32[]{:S(2)}, u32[]{:S(2)}) %collective-permute-start.4) | collective-permute-done | bytes 524320 | tf_op jit(solution)/shard_map/ppermute | solution.py:13
  155.6 4.8 %multiply_bitcast_fusion = f32[128,4,1024]{2,1,0:T(4,128)} fusion(f32[4,128,1024]{2,1,0:T(8,128)S(1)} %pad_maximum_fusion, s32[4]{0:T(128)S(1)} %bitcast.129), kind=kOutput, calls=%fused_computation.45 | convolution fusion | flops 25690128 | bytes 4194320 | tf_op jit(solution)/shard_map/dk,dlf->lkf/dot_general | solution.py:25
  162.8 3.5 %fusion.66 = f32[128,128,128]{2,0,1:T(8,128)S(1)} fusion(f32[128,32,128]{2,1,0:T(8,128)S(1)} %mul.80, s32[128]{0:T(128)S(1)} %bitcast.131), kind=kOutput, calls=%fused_computation.79 | convolution fusion | flops 805310464 | bytes 10486272 | tf_op jit(solution)/shard_map/ljb,cj->lcb/dot_general | solution.py:108
  166.4 11.0 %fusion.2 = f32[128,1,128]{2,1,0:T(1,128)S(1)} fusion(f32[128,128,128]{2,0,1:T(8,128)S(1)} %fusion.66, bf16[128,128,1]{1,0,2:T(8,128)(2,1)S(1)} %bitcast.126), kind=kOutput, calls=%fused_computation.3 | convolution fusion | flops 25165824 | bytes 8486912 | tf_op jit(solution)/shard_map/lcb,cb->lc/dot_general | solution.py:109
  177.7 5.8 %all-gather = f32[512,128]{1,0:T(8,128)S(1)} all-gather(f32[128,128]{1,0:T(8,128)S(1)} %fusion.61), channel_id=2, replica_groups=mesh['sub'=8,'grp'=4] {'grp'}, dimensions={0}, use_global_device_ids=true | all-gather | bytes 327680 | tf_op jit(solution)/shard_map/all_gather | solution.py:83
  183.5 4.7 %collective-permute-start.8 = (f32[4,128,128]{2,1,0:T(8,128)S(1)}, f32[4,128,128]{2,1,0:T(8,128)S(1)}, u32[]{:S(2)}, u32[]{:S(2)}) collective-permute-start(f32[4,128,128]{2,1,0:T(8,128)S(1)} %bitcast.121), channel_id=1, source_target_pairs={{0,28},{4,0},{8,4},{12,8},{16,12},{20,16},{24,20},{28,24},{1,29},{... | collective-permute-start | bytes 786440 | tf_op jit(solution)/shard_map/ppermute | solution.py:13
  190.2 3.6 %fusion.37 = f32[32,128,128]{2,1,0:T(8,128)} fusion(f32[128,32,128]{2,1,0:T(8,128)S(1)} %mul.80, bf16[1,32,128,128]{3,2,1,0:T(8,128)(2,1)S(1)} %copy-done.9), kind=kOutput, calls=%fused_computation.38 | convolution fusion | flops 805306368 | bytes 5242880 | tf_op jit(solution)/shard_map/ljb,jbk->ljk/dot_general | solution.py:103
  194.5 2.6 collective-permute-done.7
  197.7 3.3 %collective-permute-done.9 = f32[4,128,128]{2,1,0:T(8,128)S(1)} collective-permute-done((f32[4,128,128]{2,1,0:T(8,128)S(1)}, f32[4,128,128]{2,1,0:T(8,128)S(1)}, u32[]{:S(2)}, u32[]{:S(2)}) %collective-permute-start.9) | collective-permute-done | bytes 262176 | tf_op jit(solution)/shard_map/ppermute | solution.py:13
  204.0 5.4 %fusion.5 = f32[32,128,128]{2,0,1:T(8,128)} fusion(f32[128,128]{1,0:T(8,128)S(1)} %bitcast_convert_fusion, f32[128,128]{1,0:T(8,128)S(1)} %convolution_add_fusion, s32[128]{0:T(128)S(1)} %bitcast.132), kind=kOutput, calls=%fused_computation.6 | convolution fusion | flops 807407616 | bytes 2228736 | tf_op jit(solution)/shard_map/lcb,cj->ljb/dot_general | solution.py:116
  209.3 3.1 %copy.51 = f32[32,128,128]{1,2,0:T(8,128)} copy(f32[32,128,128]{2,0,1:T(8,128)} %fusion.5) | data formatting | bytes 4194304 | tf_op jit(solution)/shard_map/lcb,cj->ljb/dot_general | solution.py:116
  212.4 5.5 %add_multiply_fusion = f32[32,128,128]{1,2,0:T(8,128)} fusion(f32[32,128,128]{1,2,0:T(8,128)} %copy.51, f32[32,128,128]{2,1,0:T(8,128)S(1)} %copy-done.6, bf16[1,32,128,128]{3,2,1,0:T(8,128)(2,1)} %param.22), kind=kOutput, calls=%fused_computation.44 | convolution fusion | flops 806354944 | bytes 7340032 | tf_op jit(solution)/shard_map/ljk,jmk->ljm/dot_general | solution.py:104
  218.0 3.1 %copy.52 = f32[128,4,1024]{2,1,0:T(4,128)} copy(f32[128,4,1024]{0,2,1:T(8,128)} %bitcast.116) | data formatting | bytes 4194304 | tf_op jit(solution)/shard_map/reshape | solution.py:41
  221.1 3.7 %fusion.80 = f32[4,128,1024]{2,0,1:T(4,128)S(1)} fusion(f32[128,4,1024]{2,1,0:T(4,128)} %copy.52, s32[4]{0:T(128)S(1)} %bitcast.130), kind=kOutput, calls=%fused_computation.101 | convolution fusion | flops 25165840 | bytes 4194320 | tf_op jit(solution)/shard_map/dk,lkf->dlf/dot_general | solution.py:42
  228.6 11.6 %collective-permute-done.10 = f32[1,128,1024]{2,1,0:T(8,128)S(1)} collective-permute-done((f32[1,128,1024]{2,1,0:T(8,128)S(1)}, f32[1,128,1024]{2,1,0:T(8,128)S(1)}, u32[]{:S(2)}, u32[]{:S(2)}) %collective-permute-start.10) | collective-permute-done | bytes 524320 | tf_op jit(solution)/shard_map/ppermute | solution.py:13
  241.3 41.6 %psum.23 = f32[128]{0:T(128)S(1)} all-reduce(f32[128]{0:T(128)S(1)} %multiply_reduce_fusion), channel_id=1, replica_groups=mesh['sub'=8,'grp'=4] {'sub','grp'}, use_global_device_ids=true, to_apply=%region_4.5 | all-reduce | flops 128 | bytes 1024 | tf_op jit(solution)/shard_map/psum | solution.py:161
  283.0 3.6 %multiply_add_fusion = (f32[1,128,2048]{2,1,0:T(8,128)}, f32[1,128,2048]{2,1,0:T(8,128)}) fusion(f32[1,128,2048]{2,1,0:T(8,128)} %param.16, f32[1,128,1024]{2,1,0:T(8,128)} %copy-done.8, f32[1,128,1024]{2,1,0:T(8,128)} %copy-done.7, f32[128]{0:T(128)S(1)} %div.23, f32[1,128,2048]{2,1,0:T(8,128)} %param.14, f32[128]{0:T(128)S(1)} %div.18), kind=kLoop, calls=%fused_computation.57 | loop fusion | flops 1310720 | bytes 5243904 | tf_op jit(solution)/shard_map/add | solution.py:164
  (104 shorter events, 29.8 us)
Async XLA Ops:
  0.6 59.0 %copy-start = (bf16[1,96,128,128]{3,2,1,0:T(8,128)(2,1)S(1)}, bf16[1,96,128,128]{3,2,1,0:T(8,128)(2,1)}, u32[]{:S(2)}) copy-start(bf16[1,96,128,128]{3,2,1,0:T(8,128)(2,1)} %param.20) | copy-start | bytes 9437188
  0.6 20.0 %copy-start.17 = (s32[1,4]{1,0:T(1,128)S(1)}, s32[1,4]{1,0:T(1,128)}, u32[]{:S(2)}) copy-start(s32[1,4]{1,0:T(1,128)} %param.18) | copy-start | bytes 52
  2.6 18.0 %collective-permute-start = (f32[1,128,1024]{2,0,1:T(1,128)S(1)}, f32[1,128,1024]{2,0,1:T(1,128)S(1)}, u32[]{:S(2)}, u32[]{:S(2)}) collective-permute-start(f32[1,128,1024]{2,0,1:T(1,128)S(1)} %copy.70), channel_id=1, source_target_pairs={{0,4},{4,8},{8,12},{12,16},{16,20},{20,24},{24,28},{28,0},{1,5},{5... | collective-permute-start | bytes 1572872 | tf_op jit(solution)/shard_map/ppermute | solution.py:13
  6.2 14.4 %collective-permute-start.1 = (f32[1,128,1024]{2,0,1:T(1,128)S(1)}, f32[1,128,1024]{2,0,1:T(1,128)S(1)}, u32[]{:S(2)}, u32[]{:S(2)}) collective-permute-start(f32[1,128,1024]{2,0,1:T(1,128)S(1)} %copy.71), channel_id=1, source_target_pairs={{0,1},{1,2},{2,3},{3,0},{4,5},{5,6},{6,7},{7,4},{8,9},{9,10},{10,1... | collective-permute-start | bytes 1572872 | tf_op jit(solution)/shard_map/ppermute | solution.py:13
  28.9 2.2 copy-start.2
  82.3 1.6 copy-start.3
  82.3 1.9 copy-start.12
  98.2 13.2 %collective-permute-start.2 = (f32[1,128,1024]{2,1,0:T(8,128)S(1)}, f32[1,128,1024]{2,1,0:T(8,128)S(1)}, u32[]{:S(2)}, u32[]{:S(2)}) collective-permute-start(f32[1,128,1024]{2,1,0:T(8,128)S(1)} %copy.73), channel_id=1, source_target_pairs={{0,28},{4,0},{8,4},{12,8},{16,12},{20,16},{24,20},{28,24},{1,29},{... | collective-permute-start | bytes 1572872 | tf_op jit(solution)/shard_map/ppermute | solution.py:13
  100.0 11.7 %copy-start.5 = (f32[1,128,2048]{2,1,0:T(8,128)S(1)}, f32[1,128,2048]{2,1,0:T(8,128)}, u32[]{:S(2)}) copy-start(f32[1,128,2048]{2,1,0:T(8,128)} %param.16) | copy-start | bytes 3145732
  100.1 11.4 %collective-permute-start.3 = (f32[1,128,1024]{2,1,0:T(8,128)S(1)}, f32[1,128,1024]{2,1,0:T(8,128)S(1)}, u32[]{:S(2)}, u32[]{:S(2)}) collective-permute-start(f32[1,128,1024]{2,1,0:T(8,128)S(1)} %copy.75), channel_id=1, source_target_pairs={{0,3},{1,0},{2,1},{3,2},{4,7},{5,4},{6,5},{7,6},{8,11},{9,8},{10,9... | collective-permute-start | bytes 1572872 | tf_op jit(solution)/shard_map/ppermute | solution.py:13
  111.5 27.3 %copy-start.20 = (f32[128]{0:T(128)S(1)}, f32[128]{0:T(128)}, u32[]{:S(2)}) copy-start(f32[128]{0:T(128)} %param.17) | copy-start | bytes 1540
  138.7 1.7 copy-start.19
  138.7 1.7 copy-start.15
  140.1 100.3 %copy-start.4 = (f32[1,128,2048]{2,1,0:T(8,128)}, f32[1,128,2048]{2,1,0:T(8,128)S(1)}, u32[]{:S(2)}) copy-start(f32[1,128,2048]{2,1,0:T(8,128)S(1)} %multiply_subtract_fusion) | copy-start | bytes 3145732
  140.3 12.7 %copy-start.10 = (f32[1,128,1024]{2,1,0:T(8,128)}, f32[1,128,1024]{2,1,0:T(8,128)S(1)}, u32[]{:S(2)}) copy-start(f32[1,128,1024]{2,1,0:T(8,128)S(1)} %get-tuple-element.18) | copy-start | bytes 1572868
  140.3 12.7 %copy-start.11 = (f32[1,128,1024]{2,1,0:T(8,128)}, f32[1,128,1024]{2,1,0:T(8,128)S(1)}, u32[]{:S(2)}) copy-start(f32[1,128,1024]{2,1,0:T(8,128)S(1)} %get-tuple-element.19) | copy-start | bytes 1572868
  140.3 12.7 %collective-permute-start.4 = (f32[1,128,1024]{2,1,0:T(8,128)S(1)}, f32[1,128,1024]{2,1,0:T(8,128)S(1)}, u32[]{:S(2)}, u32[]{:S(2)}) collective-permute-start(f32[1,128,1024]{2,1,0:T(8,128)S(1)} %get-tuple-element.18), channel_id=1, source_target_pairs={{0,4},{4,8},{8,12},{12,16},{16,20},{20,24},{24,28},{28,0},{1,5},{5... | collective-permute-start | bytes 1572872 | tf_op jit(solution)/shard_map/ppermute | solution.py:13
  140.4 13.4 %collective-permute-start.5 = (f32[1,128,1024]{2,1,0:T(8,128)S(1)}, f32[1,128,1024]{2,1,0:T(8,128)}, u32[]{:S(2)}, u32[]{:S(2)}) collective-permute-start(f32[1,128,1024]{2,1,0:T(8,128)S(1)} %get-tuple-element.19), channel_id=1, source_target_pairs={{0,1},{1,2},{2,3},{3,0},{4,5},{5,6},{6,7},{7,4},{8,9},{9,10},{10,1... | collective-permute-start | bytes 1572872 | tf_op jit(solution)/shard_map/ppermute | solution.py:13
  160.3 2.5 copy-start.18
  166.4 11.0 %copy-start.16 = (f32[1,128,128]{2,1,0:T(8,128)S(1)}, f32[1,128,128]{2,1,0:T(8,128)}, u32[]{:S(2)}) copy-start(f32[1,128,128]{2,1,0:T(8,128)} %param.26) | copy-start | bytes 196612
  166.4 23.8 %copy-start.9 = (bf16[1,32,128,128]{3,2,1,0:T(8,128)(2,1)S(1)}, bf16[1,32,128,128]{3,2,1,0:T(8,128)(2,1)}, u32[]{:S(2)}) copy-start(bf16[1,32,128,128]{3,2,1,0:T(8,128)(2,1)} %param.22) | copy-start | bytes 3145732
  183.5 11.0 %collective-permute-start.6 = (f32[4,128,128]{2,1,0:T(8,128)S(1)}, f32[4,128,128]{2,1,0:T(8,128)S(1)}, u32[]{:S(2)}, u32[]{:S(2)}) collective-permute-start(f32[4,128,128]{2,1,0:T(8,128)S(1)} %bitcast.119), channel_id=1, source_target_pairs={{0,8},{4,12},{8,16},{12,20},{16,24},{20,28},{24,0},{28,4},{1,9},{5... | collective-permute-start | bytes 786440 | tf_op jit(solution)/shard_map/ppermute | solution.py:13
  183.5 13.7 %collective-permute-start.7 = (f32[4,128,128]{2,1,0:T(8,128)S(1)}, f32[4,128,128]{2,1,0:T(8,128)S(1)}, u32[]{:S(2)}, u32[]{:S(2)}) collective-permute-start(f32[4,128,128]{2,1,0:T(8,128)S(1)} %bitcast.120), channel_id=1, source_target_pairs={{0,4},{4,8},{8,12},{12,16},{16,20},{20,24},{24,28},{28,0},{1,5},{5... | collective-permute-start | bytes 786440 | tf_op jit(solution)/shard_map/ppermute | solution.py:13
  183.5 14.2 %collective-permute-start.8 = (f32[4,128,128]{2,1,0:T(8,128)S(1)}, f32[4,128,128]{2,1,0:T(8,128)S(1)}, u32[]{:S(2)}, u32[]{:S(2)}) collective-permute-start(f32[4,128,128]{2,1,0:T(8,128)S(1)} %bitcast.121), channel_id=1, source_target_pairs={{0,28},{4,0},{8,4},{12,8},{16,12},{20,16},{24,20},{28,24},{1,29},{... | collective-permute-start | bytes 786440 | tf_op jit(solution)/shard_map/ppermute | solution.py:13
  188.2 12.9 %collective-permute-start.9 = (f32[4,128,128]{2,1,0:T(8,128)S(1)}, f32[4,128,128]{2,1,0:T(8,128)S(1)}, u32[]{:S(2)}, u32[]{:S(2)}) collective-permute-start(f32[4,128,128]{2,1,0:T(8,128)S(1)} %bitcast.122), channel_id=1, source_target_pairs={{0,24},{4,28},{8,0},{12,4},{16,8},{20,12},{24,16},{28,20},{1,25},{... | collective-permute-start | bytes 786440 | tf_op jit(solution)/shard_map/ppermute | solution.py:13
  197.2 5.3 %copy-start.13 = (f32[1,9,128,128]{3,2,1,0:T(8,128)S(1)}, f32[1,9,128,128]{3,2,1,0:T(8,128)}, u32[]{:S(2)}) copy-start(f32[1,9,128,128]{3,2,1,0:T(8,128)} %param.25) | copy-start | bytes 1769476
  209.3 3.1 %copy-start.6 = (f32[32,128,128]{2,1,0:T(8,128)S(1)}, f32[32,128,128]{2,1,0:T(8,128)}, u32[]{:S(2)}) copy-start(f32[32,128,128]{2,1,0:T(8,128)} %fusion.37) | copy-start | bytes 6291460
  226.4 13.8 %collective-permute-start.10 = (f32[1,128,1024]{2,1,0:T(8,128)S(1)}, f32[1,128,1024]{2,1,0:T(8,128)S(1)}, u32[]{:S(2)}, u32[]{:S(2)}) collective-permute-start(f32[1,128,1024]{2,1,0:T(8,128)S(1)} %copy.77), channel_id=1, source_target_pairs={{0,28},{4,0},{8,4},{12,8},{16,12},{20,16},{24,20},{28,24},{1,29},{... | collective-permute-start | bytes 1572872 | tf_op jit(solution)/shard_map/ppermute | solution.py:13
  228.0 12.3 %collective-permute-start.11 = (f32[1,128,1024]{2,1,0:T(8,128)S(1)}, f32[1,128,1024]{2,1,0:T(8,128)S(1)}, u32[]{:S(2)}, u32[]{:S(2)}) collective-permute-start(f32[1,128,1024]{2,1,0:T(8,128)S(1)} %copy.79), channel_id=1, source_target_pairs={{0,3},{1,0},{2,1},{3,2},{4,7},{5,4},{6,5},{7,6},{8,11},{9,8},{10,9... | collective-permute-start | bytes 1572872 | tf_op jit(solution)/shard_map/ppermute | solution.py:13
  240.5 0.8 copy-start.8
  283.0 3.6 %copy-start.21 = (f32[128]{0:T(128)}, f32[128]{0:T(128)S(1)}, u32[]{:S(2)}) copy-start(f32[128]{0:T(128)S(1)} %psum.23) | copy-start | bytes 1540
  283.0 3.6 %copy-start.1 = (bf16[1,96,128,128]{3,2,1,0:T(8,128)(2,1)S(1)}, bf16[1,96,128,128]{3,2,1,0:T(8,128)(2,1)}, u32[]{:S(2)}) copy-start(bf16[1,96,128,128]{3,2,1,0:T(8,128)(2,1)} %param.20) | copy-start | bytes 9437188
  (2 other events, 1.6 us)
